TPU v7x, 32 devices: a whole 2x2x4 slice. The times are simulated.
32 devices in a mesh: pts: 8 (over z, x), grp: 4 (over y, core).
Axes of the slice: x: 2, y: 2, z: 4, core: 2. Of those that a mesh axis runs over, the one named last changes fastest.
Arguments:
- embeddings: bfloat16 [131072, 1024], P(('pts', 'grp')), as said below
- best_start: float32 [131072], P(('pts', 'grp')), may hold values from 0 to 2
- bounds_start: float32 [131072], P(('pts', 'grp')), may hold values from 0 to 4
- proposals: int32 [8, 32], replicated, may hold values from 0 to 131071
Outputs:
- gain_table: float32 [8, 32], replicated
- coverage: float32 [8], replicated
- best_final: float32 [131072], P(('pts', 'grp'))
- bounds_final: float32 [131072], P(('pts', 'grp'))
Inputs may be any that keep to these rules, and one draw needn't show every extreme that they name: Rows are real valued embeddings of varying norm.
All inputs are finite; a program needn't handle non-finite values.
Results may differ from a plain program's by a relative error of at most 0.0003.
Values may be sent and summed in bfloat16 or wider, within the bound.
A program may use at most 64 MiB of HBM per device.

v0:
```python
import jax
import jax.numpy as jnp
from jax import lax
from jax.sharding import PartitionSpec as P

STEPS = 8


def on_device(embeddings, best_start, bounds_start, proposals):
    row_count = embeddings.shape[0]
    prop_count = proposals.shape[1]
    own_index = lax.axis_index(("pts", "grp"))
    first_row = own_index * row_count
    point_total = row_count * lax.axis_size(("pts", "grp"))
    local_ids = first_row + jnp.arange(row_count, dtype=jnp.int32)
    best_sim = best_start
    bounds = bounds_start
    gain_rows = []
    cover_rows = []
    flat_chosen = proposals.reshape(-1)
    flat_offset = flat_chosen - first_row
    flat_owned = (flat_offset >= 0) & (flat_offset < row_count)
    all_rows = jnp.take(embeddings, jnp.clip(flat_offset, 0, row_count - 1), axis=0)
    all_masked = jnp.where(flat_owned[:, None], all_rows, jnp.zeros_like(all_rows)).astype(
        jnp.float32
    )
    fetched_all = lax.psum(all_masked, ("pts", "grp")).astype(jnp.bfloat16)
    similarity_all = lax.dot_general(
        embeddings, fetched_all, (((1,), (1,)), ((), ())), preferred_element_type=jnp.float32
    )
    for step_index in range(STEPS):
        chosen = proposals[step_index]
        similarity = similarity_all[:, step_index * prop_count : (step_index + 1) * prop_count]
        clipped = jnp.maximum(similarity - best_sim[:, None], 0.0)
        partial_sums = jnp.sum(clipped, axis=0)
        gain_values = lax.psum(partial_sums, ("pts", "grp")) / point_total
        weights = (gain_values + 0.01) / (jnp.sum(gain_values) + 0.01 * prop_count)
        mixed = jnp.dot(similarity, weights, precision=lax.Precision.HIGHEST)
        best_sim = jnp.maximum(best_sim, mixed)
        cover_rows.append(lax.psum(jnp.sum(best_sim), ("pts", "grp")) / point_total)
        matches = local_ids[:, None] == chosen[None, :]
        refreshed = jnp.max(jnp.where(matches, gain_values[None, :], -1.0), axis=1)
        bounds = jnp.where(jnp.any(matches, axis=1), refreshed, bounds)
        gain_rows.append(gain_values)
    return (jnp.stack(gain_rows), jnp.stack(cover_rows), best_sim, bounds)


def solution(mesh):
    placed = (P(("pts", "grp"), None), P(("pts", "grp")), P(("pts", "grp")), P())
    return jax.shard_map(
        on_device,
        mesh=mesh,
        in_specs=placed,
        out_specs=(P(), P(), P(("pts", "grp")), P(("pts", "grp"))),
        check_vma=False,
    )
```

profile of v0, /device:TPU:0, one launch (start us, length us, event | category | flops | bytes accessed | tf_op | source)
XLA Modules:
  0.0 473.4 jit_solution(3717555113697132605)
XLA Ops:
  1.5 6.0 %gather_fusion = bf16[256,1024]{1,0:T(8,128)(2,1)S(1)} fusion(bf16[4096,1024]{1,0:T(8,128)(2,1)} %param.4, s32[1024]{0:T(1024)S(1)} %pad_clamp_fusion), kind=kCustom, calls=%fused_computation | custom fusion | bytes 1049600 | tf_op jit(solution)/shard_map/jit(_take)/gather | solution.py:23
  7.9 53.3 %all-reduce.2 = bf16[256,1024]{1,0:T(8,128)(2,1)S(1)} all-reduce(f32[256,1024]{1,0:T(8,128)S(1)} %select_convert_fusion), channel_id=1, replica_groups=mesh['pts'=8,'grp'=4] {'pts','grp'}, use_global_device_ids=true, to_apply=%region_0.1 | all-reduce | flops 262144 | bytes 1572864 | tf_op jit(solution)/shard_map/psum | solution.py:27
  61.2 7.7 %convolution_bitcast_fusion = f32[4096,256]{0,1:T(8,128)} fusion(bf16[4096,1024]{1,0:T(8,128)(2,1)} %param.4, bf16[256,1024]{1,0:T(8,128)(2,1)S(1)} %all-reduce.2), kind=kOutput, calls=%fused_computation.1 | convolution fusion | flops 2147483648 | bytes 13107200 | tf_op jit(solution)/shard_map/dot_general | solution.py:28
  68.9 1.2 maximum_reduce_fusion.7
  70.1 38.8 %psum.120 = f32[32]{0:T(128)S(1)} all-reduce(f32[32]{0:T(128)S(1)} %maximum_reduce_fusion.7), channel_id=1, replica_groups=mesh['pts'=8,'grp'=4] {'pts','grp'}, use_global_device_ids=true, to_apply=%region_2.3 | all-reduce | flops 32 | bytes 256 | tf_op jit(solution)/shard_map/psum | solution.py:36
  110.2 1.4 fusion.23
  112.2 1.2 maximum_reduce_fusion.6
  113.4 39.3 %psum.121 = f32[32]{0:T(128)S(1)} all-reduce(f32[32]{0:T(128)S(1)} %maximum_reduce_fusion.6), channel_id=1, replica_groups=mesh['pts'=8,'grp'=4] {'pts','grp'}, use_global_device_ids=true, to_apply=%region_5.6 | all-reduce | flops 32 | bytes 256 | tf_op jit(solution)/shard_map/psum | solution.py:36
  154.0 1.4 fusion.21
  156.0 1.2 maximum_reduce_fusion.5
  157.2 40.6 %psum.122 = f32[32]{0:T(128)S(1)} all-reduce(f32[32]{0:T(128)S(1)} %maximum_reduce_fusion.5), channel_id=1, replica_groups=mesh['pts'=8,'grp'=4] {'pts','grp'}, use_global_device_ids=true, to_apply=%region_8.9 | all-reduce | flops 32 | bytes 256 | tf_op jit(solution)/shard_map/psum | solution.py:36
  199.1 1.4 fusion.19
  202.3 39.3 %psum.123 = f32[32]{0:T(128)S(1)} all-reduce(f32[32]{0:T(128)S(1)} %maximum_reduce_fusion.4), channel_id=1, replica_groups=mesh['pts'=8,'grp'=4] {'pts','grp'}, use_global_device_ids=true, to_apply=%region_11.12 | all-reduce | flops 32 | bytes 256 | tf_op jit(solution)/shard_map/psum | solution.py:36
  242.9 1.4 fusion.17
  246.2 40.6 %psum.124 = f32[32]{0:T(128)S(1)} all-reduce(f32[32]{0:T(128)S(1)} %maximum_reduce_fusion.3), channel_id=1, replica_groups=mesh['pts'=8,'grp'=4] {'pts','grp'}, use_global_device_ids=true, to_apply=%region_14.15 | all-reduce | flops 32 | bytes 256 | tf_op jit(solution)/shard_map/psum | solution.py:36
  288.0 1.4 fusion.15
  291.3 39.5 %psum.125 = f32[32]{0:T(128)S(1)} all-reduce(f32[32]{0:T(128)S(1)} %maximum_reduce_fusion.2), channel_id=1, replica_groups=mesh['pts'=8,'grp'=4] {'pts','grp'}, use_global_device_ids=true, to_apply=%region_17.18 | all-reduce | flops 32 | bytes 256 | tf_op jit(solution)/shard_map/psum | solution.py:36
  332.1 1.4 fusion.13
  335.3 40.6 %psum.126 = f32[32]{0:T(128)S(1)} all-reduce(f32[32]{0:T(128)S(1)} %maximum_reduce_fusion.1), channel_id=1, replica_groups=mesh['pts'=8,'grp'=4] {'pts','grp'}, use_global_device_ids=true, to_apply=%region_20.21 | all-reduce | flops 32 | bytes 256 | tf_op jit(solution)/shard_map/psum | solution.py:36
  377.2 1.4 fusion.11
  380.4 39.3 %psum.127 = f32[32]{0:T(128)S(1)} all-reduce(f32[32]{0:T(128)S(1)} %maximum_reduce_fusion), channel_id=1, replica_groups=mesh['pts'=8,'grp'=4] {'pts','grp'}, use_global_device_ids=true, to_apply=%region_23.24 | all-reduce | flops 32 | bytes 256 | tf_op jit(solution)/shard_map/psum | solution.py:36
  423.3 1.4 fusion.9
  424.7 1.2 fusion.89
  425.9 41.2 %all-reduce = (f32[]{:T(128)}, f32[]{:T(128)}, f32[]{:T(128)}, f32[]{:T(128)}, f32[]{:T(128)}, /*index=5*/f32[]{:T(128)}, f32[]{:T(128)}, f32[]{:T(128)}) all-reduce(f32[]{:T(128)} %get-tuple-element.42, f32[]{:T(128)} %get-tuple-element.40, f32[]{:T(128)} %get-tuple-element.38, ...), channel_id=1, replica_groups=mesh['pts'=8,'grp'=4] {'pts','grp'}, use_global_device_ids=true, to_apply=%region_25.26 | all-reduce | flops 8 | bytes 64 | tf_op jit(solution)/shard_map/psum | solution.py:40
  (42 shorter events, 19.8 us)
Async XLA Ops:
  0.6 7.0 %copy-start.1 = (s32[8,32]{1,0:T(8,128)S(1)}, s32[8,32]{1,0:T(8,128)}, u32[]{:S(2)}) copy-start(s32[8,32]{1,0:T(8,128)} %param.7) | copy-start | bytes 3076
  61.2 7.7 %copy-start = (f32[4096]{0:T(1024)S(1)}, f32[4096]{0:T(1024)}, u32[]{:S(2)}) copy-start(f32[4096]{0:T(1024)} %param.5) | copy-start | bytes 49156
  70.1 351.9 %copy-start.2 = (f32[4096]{0:T(1024)S(1)}, f32[4096]{0:T(1024)}, u32[]{:S(2)}) copy-start(f32[4096]{0:T(1024)} %param.6) | copy-start | bytes 49156
where the time goes:
time: 475 us; the launch traced here: 473 us
  blocking collectives  413 us (87%)
  other arithmetic  23.2 us (5%)
  matrix products  19.1 us (4%)
  between operations  11.1 us (2%)
  local copies, waits for them, and re-layouts  7.49 us (2%)
    psum x8, blocking collectives, on_device(): gain_values = lax.psum(partial_sums, ('pts', 'grp')) / point_total  318 us
    psum x1, blocking collectives, on_device(): fetched_all = lax.psum(all_masked, ('pts', 'grp')).astype(jnp.bfloat16)  53.3 us
    psum x1, blocking collectives, on_device(): cover_rows.append(lax.psum(jnp.sum(best_sim), ('pts', 'grp')) / point_total)  41.2 us
    dot_general x8, matrix products, on_device(): mixed = jnp.dot(similarity, weights, precision=lax.Precision.HIGHEST)  11.4 us
    reduce_sum x8, other arithmetic, on_device(): partial_sums = jnp.sum(clipped, axis=0)  9.6 us

commit v1 on v0

v1 whole, which is shorter than its diff:
```python
import functools

import jax
import jax.numpy as jnp
from jax import lax
from jax.experimental import pallas as pl
from jax.experimental.pallas import tpu as pltpu
from jax.sharding import PartitionSpec as P

LANES = 128
SUBLANES = 8
LOAD_CHUNKS = 8
MESH = pl.DeviceIdType.MESH


def greedy_kernel(
    pts, grp, steps, props, rows, width,
    emb_hbm, best_in, bounds_in, props_in,
    gain_out, cover_out, best_out, bounds_out,
    emb, load_sem, chosen, picked, arrived, block_sum, fetched, sims, gain_src, gain_buf,
    cover_part, gain_col,
    rs_send, rs_recv, ag_send, ag_recv, gain_send, gain_recv,
):
    n = pts * grp
    blocks = (props // SUBLANES) * (width // LANES)
    spread = n // blocks
    across = width // LANES
    point_total = rows * n
    me = lax.axis_index("pts") * grp + lax.axis_index("grp")
    first_row = me * rows
    my_block = me if spread == 1 else me // spread
    is_owner = None if spread == 1 else lax.rem(me, spread) == 0

    def coords(device):
        return (device // grp, lax.rem(device, grp))

    chunk = rows // LOAD_CHUNKS
    loads = [
        pltpu.make_async_copy(
            emb_hbm.at[pl.ds(i * chunk, chunk)], emb.at[pl.ds(i * chunk, chunk)], load_sem.at[i]
        )
        for i in range(LOAD_CHUNKS)
    ]
    for load in loads:
        load.start()

    barrier = pltpu.get_barrier_semaphore()

    @pl.loop(1, n)
    def _(hop):
        pl.semaphore_signal(
            barrier, inc=1, device_id=coords(lax.rem(me + hop, n)), device_id_type=MESH
        )

    eye = lax.broadcasted_iota(jnp.int32, (props, LANES), 0) == lax.broadcasted_iota(
        jnp.int32, (props, LANES), 1
    )
    small_eye = lax.broadcasted_iota(jnp.int32, (props, props), 0) == lax.broadcasted_iota(
        jnp.int32, (props, props), 1
    )
    lane = lax.broadcasted_iota(jnp.int32, (1, LANES), 1)
    for s in range(steps):
        offsets = (props_in[pl.ds(s, 1), :] - first_row).astype(jnp.float32)
        column = jnp.sum(jnp.where(small_eye, offsets, 0.0), axis=1, keepdims=True)
        chosen[s] = jnp.broadcast_to(column, (props, LANES)).astype(jnp.int32)

    best_out[...] = best_in[...]
    bounds_out[...] = bounds_in[...]
    cover_part[...] = jnp.zeros_like(cover_part)

    def pick(low, high):
        ids = lax.broadcasted_iota(jnp.int32, (props, rows), 1)
        hot = [
            jnp.where(ids == chosen[s][:, :1], 1.0, 0.0).astype(jnp.bfloat16)
            for s in range(low, high)
        ]
        hot = jnp.concatenate(hot, axis=0)
        for c in range(width // (2 * LANES)):
            part = jnp.dot(
                hot,
                emb[:, c * 2 * LANES : (c + 1) * 2 * LANES],
                preferred_element_type=jnp.float32,
            )
            for s in range(low, high):
                for r in range(props // SUBLANES):
                    for h in range(2):
                        top = (s - low) * props + r * SUBLANES
                        picked[s, r * across + 2 * c + h] = part[
                            top : top + SUBLANES, h * LANES : (h + 1) * LANES
                        ].astype(jnp.bfloat16)

    def scatter(s):
        def to(block, device):
            hop = lax.rem(device - me + n, n)
            pltpu.make_async_remote_copy(
                src_ref=picked.at[s, block],
                dst_ref=arrived.at[s, hop - 1],
                send_sem=rs_send.at[s],
                recv_sem=rs_recv.at[s],
                device_id=coords(device),
                device_id_type=MESH,
            ).start()

        if spread == 1:

            @pl.loop(1, n)
            def _(hop):
                device = lax.rem(me + hop, n)
                to(device, device)
        else:

            @pl.loop(0, blocks)
            def _(block):
                @pl.when(block * spread != me)
                def _():
                    to(block, block * spread)

    def wait_for(ref, sem):
        pltpu.make_async_copy(ref, ref, sem).wait()

    def when_owner(f):
        if spread == 1:
            f()
        else:
            pl.when(is_owner)(f)

    def gather(s):
        @when_owner
        def _():
            wait_for(arrived.at[s], rs_recv.at[s])
            total = jnp.sum(arrived[s].astype(jnp.float32), axis=0)
            total = (total + picked[s, my_block].astype(jnp.float32)).astype(jnp.bfloat16)
            block_sum[s] = total
            fetched[s, my_block] = total

            @pl.loop(1, n)
            def _(hop):
                pltpu.make_async_remote_copy(
                    src_ref=block_sum.at[s],
                    dst_ref=fetched.at[s, my_block],
                    send_sem=ag_send.at[s],
                    recv_sem=ag_recv.at[s],
                    device_id=coords(lax.rem(me + hop, n)),
                    device_id_type=MESH,
                ).start()

    def similarity(s):
        if spread == 1:
            wait_for(fetched.at[s, pl.ds(0, blocks - 1)], ag_recv.at[s])
        else:

            @pl.when(is_owner)
            def _():
                wait_for(fetched.at[s, pl.ds(0, blocks - 1)], ag_recv.at[s])

            @pl.when(jnp.logical_not(is_owner))
            def _():
                wait_for(fetched.at[s], ag_recv.at[s])

        lines = []
        for r in range(props // SUBLANES):
            lines.append(
                jnp.concatenate(
                    [fetched[s, r * across + c].astype(jnp.float32) for c in range(across)], axis=1
                )
            )
        wanted = jnp.concatenate(lines, axis=0).astype(jnp.bfloat16)
        slot = lax.rem(s, 2)
        piece = 512
        for i in range(rows // piece):
            sims[slot, :, i * piece : (i + 1) * piece] = lax.dot_general(
                wanted,
                emb[i * piece : (i + 1) * piece, :],
                (((1,), (1,)), ((), ())),
                preferred_element_type=jnp.float32,
            )

    def send_sums(s, row):
        gain_src[s] = row
        gain_buf[s, me] = row

        @pl.loop(1, n)
        def _(hop):
            pltpu.make_async_remote_copy(
                src_ref=gain_src.at[s],
                dst_ref=gain_buf.at[s, me],
                send_sem=gain_send.at[s],
                recv_sem=gain_recv.at[s],
                device_id=coords(lax.rem(me + hop, n)),
                device_id_type=MESH,
            ).start()

    def take_sums(s):
        wait_for(gain_buf.at[s, pl.ds(0, n - 1)], gain_recv.at[s])
        return jnp.sum(gain_buf[s], axis=0) / point_total

    def refresh(s):
        gains = gain_col[...]
        ours = chosen[s]
        for i in range(rows // LANES):
            at = slice(i * LANES, (i + 1) * LANES)
            match = ours == lax.broadcasted_iota(jnp.int32, (props, LANES), 1) + i * LANES
            value = jnp.max(jnp.where(match, gains, -1.0), axis=0, keepdims=True)
            bounds_out[:, at] = jnp.where(value >= 0.0, value, bounds_out[:, at])

    def keep_cover(s, means):
        value = jnp.sum(jnp.where(lane == props, means, 0.0), axis=1, keepdims=True)
        cover_out[...] = jnp.where(lane[:, :steps] == s, value, cover_out[...])

    cover_out[...] = jnp.zeros_like(cover_out)
    early = min(2, steps)
    for load in loads:
        load.wait()
    pick(0, early)
    pl.semaphore_wait(barrier, n - 1)
    for s in range(early):
        scatter(s)
    pick(early, steps)
    for s in range(early):
        gather(s)
    scatter(early)
    similarity(0)

    @pl.loop(0, steps)
    def _(s):
        slot = lax.rem(s, 2)
        clipped = jnp.zeros((props, LANES), jnp.float32)
        for i in range(rows // LANES):
            at = slice(i * LANES, (i + 1) * LANES)
            clipped += jnp.maximum(sims[slot, :, at] - best_out[:, at], 0.0)
        column = jnp.sum(clipped, axis=1, keepdims=True)
        row = jnp.sum(jnp.where(eye, column, 0.0), axis=0, keepdims=True)
        cover = jnp.sum(cover_part[...], axis=1, keepdims=True)
        send_sums(s, jnp.where(lane == props, cover, row))

        @pl.when(s + 2 < steps)
        def _():
            gather(s + 2)

        @pl.when(s + 3 < steps)
        def _():
            scatter(s + 3)

        @pl.when(s > 0)
        def _():
            refresh(s - 1)

        @pl.when(s + 1 < steps)
        def _():
            similarity(s + 1)

        means = take_sums(s)
        gains = jnp.sum(jnp.where(eye, means, 0.0), axis=1, keepdims=True)
        weights = (gains + 0.01) / (jnp.sum(gains, axis=0, keepdims=True) + 0.01 * props)
        weights = jnp.broadcast_to(weights, (props, LANES))
        covered = jnp.zeros((1, LANES), jnp.float32)
        for i in range(rows // LANES):
            at = slice(i * LANES, (i + 1) * LANES)
            mixed = jnp.sum(sims[slot, :, at] * weights, axis=0, keepdims=True)
            best = jnp.maximum(best_out[:, at], mixed)
            best_out[:, at] = best
            covered += best
        cover_part[...] = covered
        gain_col[...] = jnp.broadcast_to(gains, (props, LANES))
        gain_out[pl.ds(s, 1), :] = means[:, :props]

        @pl.when(s > 0)
        def _():
            keep_cover(s - 1, means)

    cover = jnp.sum(cover_part[...], axis=1, keepdims=True)
    send_sums(steps, jnp.where(lane == props, cover, 0.0))
    refresh(steps - 1)
    keep_cover(steps - 1, take_sums(steps))

    @pl.loop(0, steps)
    def _(s):
        if spread == 1:
            wait_for(picked.at[s, pl.ds(0, blocks - 1)], rs_send.at[s])
            wait_for(arrived.at[s], ag_send.at[s])
        else:

            @pl.when(is_owner)
            def _():
                wait_for(picked.at[s, pl.ds(0, blocks - 1)], rs_send.at[s])
                wait_for(arrived.at[s], ag_send.at[s])

            @pl.when(jnp.logical_not(is_owner))
            def _():
                wait_for(picked.at[s], rs_send.at[s])

    @pl.loop(0, steps + 1)
    def _(s):
        wait_for(gain_buf.at[s, pl.ds(0, n - 1)], gain_send.at[s])


def on_device(pts, grp, embeddings, best_start, bounds_start, proposals):
    rows, width = embeddings.shape
    steps, props = proposals.shape
    n = pts * grp
    blocks = (props // SUBLANES) * (width // LANES)
    vmem = pl.BlockSpec(memory_space=pltpu.VMEM)
    dma = pltpu.SemaphoreType.DMA
    f32, bf16 = jnp.float32, jnp.bfloat16
    gains, cover, best, bounds = pl.pallas_call(
        functools.partial(greedy_kernel, pts, grp, steps, props, rows, width),
        out_shape=(
            jax.ShapeDtypeStruct((steps, props), f32),
            jax.ShapeDtypeStruct((1, steps), f32),
            jax.ShapeDtypeStruct((1, rows), f32),
            jax.ShapeDtypeStruct((1, rows), f32),
        ),
        in_specs=[pl.BlockSpec(memory_space=pl.ANY), vmem, vmem, vmem],
        out_specs=(vmem, vmem, vmem, vmem),
        scratch_shapes=[
            pltpu.VMEM((rows, width), bf16),
            dma((LOAD_CHUNKS,)),
            pltpu.VMEM((steps, props, LANES), jnp.int32),
            pltpu.VMEM((steps, blocks, SUBLANES, LANES), bf16),
            pltpu.VMEM((steps, n - 1, SUBLANES, LANES), bf16),
            pltpu.VMEM((steps, SUBLANES, LANES), bf16),
            pltpu.VMEM((steps, blocks, SUBLANES, LANES), bf16),
            pltpu.VMEM((2, props, rows), f32),
            pltpu.VMEM((steps + 1, 1, LANES), f32),
            pltpu.VMEM((steps + 1, n, 1, LANES), f32),
            pltpu.VMEM((1, LANES), f32),
            pltpu.VMEM((props, LANES), f32),
            dma((steps,)),
            dma((steps,)),
            dma((steps,)),
            dma((steps,)),
            dma((steps + 1,)),
            dma((steps + 1,)),
        ],
        compiler_params=pltpu.CompilerParams(
            collective_id=0, has_side_effects=True, vmem_limit_bytes=56 * 1024 * 1024
        ),
    )(embeddings, best_start.reshape(1, rows), bounds_start.reshape(1, rows), proposals)
    return gains, cover.reshape(steps), best.reshape(rows), bounds.reshape(rows)


def solution(mesh):
    placed = (P(("pts", "grp"), None), P(("pts", "grp")), P(("pts", "grp")), P())
    return jax.shard_map(
        functools.partial(on_device, mesh.shape["pts"], mesh.shape["grp"]),
        mesh=mesh,
        in_specs=placed,
        out_specs=(P(), P(), P(("pts", "grp")), P(("pts", "grp"))),
        check_vma=False,
    )
```

time: 475 us -> 77.9 us (0.16)
  blocking collectives: 413 us -> 0 us
  Pallas kernels: 0 us -> 71.7 us
  other arithmetic: 23.2 us -> 0 us
  matrix products: 19.1 us -> 0 us
  between operations: 11.1 us -> 0.64 us
    psum x10 -> x0, blocking collectives: 413 us -> none  [the longest x8 318 us: on_device(): gain_values = lax.psum(partial_sums, ('pts', 'grp')) / point_total]
    pallas_call x0 -> x1, Pallas kernels: none -> 71.7 us  [on_device(): pl.pallas_call(functools.partial(greedy_kernel, pts, grp, steps, props, r...]
    dot_general x9 -> x0, matrix products: 19.1 us -> none  [the longest x8 11.4 us: on_device(): mixed = jnp.dot(similarity, weights, precision=lax.Precision.HIGHEST)]
    reduce_sum x16 -> x0, other arithmetic: 15.1 us -> none  [the longest x8 9.6 us: on_device(): partial_sums = jnp.sum(clipped, axis=0)]
    gather x1 -> x0, local copies, waits for them, and re-layouts: 6.02 us -> none  [on_device(): jnp.take(embeddings, jnp.clip(flat_offset, 0, row_count - 1), axis=0)]
    unnamed x6 -> x4, local copies, waits for them, and re-layouts: 0.01 us -> 5.06 us
    div x8 -> x0, other arithmetic: 4.8 us -> none  [on_device(): gain_values = lax.psum(partial_sums, ('pts', 'grp')) / point_total]
where the time goes in v1:
time: 77.9 us; the launch traced here: 77.4 us
  Pallas kernels  71.7 us (92%)
  local copies, waits for them, and re-layouts  5.06 us (6%)
    pallas_call x1, Pallas kernels, on_device(): pl.pallas_call(functools.partial(greedy_kernel, pts, grp, steps, props, r...  71.7 us
    unnamed x4, local copies, waits for them, and re-layouts  5.06 us

profile of v1, /device:TPU:0, one launch (start us, length us, event | category | flops | bytes accessed | tf_op | source)
XLA Modules:
  0.0 77.4 jit_solution(7032473353963292143)
XLA Ops:
  0.6 71.7 %shard_map.75 = (f32[8,32]{1,0:T(8,128)}, f32[1,8]{1,0:T(1,128)}, f32[1,4096]{1,0:T(1,128)}, f32[1,4096]{1,0:T(1,128)}) custom-call(bf16[4096,1024]{1,0:T(8,128)(2,1)} %emb_hbm.1, f32[1,4096]{1,0:T(1,128)} %bitcast.5, f32[1,4096]{1,0:T(1,128)} %bitcast.6, s32[8,32]{1,0:T(8,128)} %props_in.1), custom_call_target="tpu_custom_call" | custom-call | tf_op jit(solution)/shard_map/pallas_call | solution.py:305
  72.4 1.3 %copy.12 = f32[8,32]{1,0:T(8,128)} copy(f32[8,32]{1,0:T(8,128)} %get-tuple-element.16) | data formatting | bytes 2048
  73.6 1.1 %copy.13 = f32[8]{0:T(128)} copy(f32[8]{0:T(128)} %bitcast.9) | data formatting | bytes 64
  74.8 1.3 %copy.14 = f32[4096]{0:T(1024)} copy(f32[4096]{0:T(1024)} %bitcast.8) | data formatting | bytes 32768
  76.1 1.3 %copy.15 = f32[4096]{0:T(1024)} copy(f32[4096]{0:T(1024)} %bitcast.7) | data formatting | bytes 32768

commit v2 on v1

--- a/solution.py
+++ b/solution.py
@@ -10,6 +10,7 @@
 LANES = 128
 SUBLANES = 8
 LOAD_CHUNKS = 8
+UNROLLED_PEERS = 32
 MESH = pl.DeviceIdType.MESH
 
 
@@ -18,7 +19,7 @@
     emb_hbm, best_in, bounds_in, props_in,
     gain_out, cover_out, best_out, bounds_out,
     emb, load_sem, chosen, picked, arrived, block_sum, fetched, sims, gain_src, gain_buf,
-    cover_part, gain_col,
+    gain_col, found,
     rs_send, rs_recv, ag_send, ag_recv, gain_send, gain_recv,
 ):
     n = pts * grp
@@ -31,8 +32,34 @@
     my_block = me if spread == 1 else me // spread
     is_owner = None if spread == 1 else lax.rem(me, spread) == 0
 
+    my_pts, my_grp = lax.axis_index("pts"), lax.axis_index("grp")
+
+    def flip(position, size, step):
+        if size & (size - 1):
+            return lax.rem(position + step, size)
+        for bit in [1 << k for k in range(size.bit_length()) if step >> k & 1]:
+            position = position + bit - 2 * bit * lax.rem(position // bit, 2)
+        return position
+
+    grp_at = [flip(my_grp, grp, step) for step in range(grp)]
+
     def coords(device):
         return (device // grp, lax.rem(device, grp))
+
+    def each_peer(f):
+        def line(at, step, skip):
+            for turn in range(grp - 1, skip - 1, -1):
+                f((at, grp_at[turn]), step * grp + turn - 1)
+
+        if n <= UNROLLED_PEERS:
+            for step in range(pts - 1, 0, -1):
+                line(pts_at[step], step, 0)
+        else:
+            pl.loop(1, pts)(lambda step: line(lax.rem(my_pts + step, pts), step, 0))
+        line(my_pts, 0, 1)
+
+    if n <= UNROLLED_PEERS:
+        pts_at = [flip(my_pts, pts, step) for step in range(pts)]
 
     chunk = rows // LOAD_CHUNKS
     loads = [
@@ -46,11 +73,9 @@
 
     barrier = pltpu.get_barrier_semaphore()
 
-    @pl.loop(1, n)
-    def _(hop):
-        pl.semaphore_signal(
-            barrier, inc=1, device_id=coords(lax.rem(me + hop, n)), device_id_type=MESH
-        )
+    each_peer(
+        lambda peer, _: pl.semaphore_signal(barrier, inc=1, device_id=peer, device_id_type=MESH)
+    )
 
     eye = lax.broadcasted_iota(jnp.int32, (props, LANES), 0) == lax.broadcasted_iota(
         jnp.int32, (props, LANES), 1
@@ -66,54 +91,58 @@
 
     best_out[...] = best_in[...]
     bounds_out[...] = bounds_in[...]
-    cover_part[...] = jnp.zeros_like(cover_part)
-
-    def pick(low, high):
-        ids = lax.broadcasted_iota(jnp.int32, (props, rows), 1)
-        hot = [
-            jnp.where(ids == chosen[s][:, :1], 1.0, 0.0).astype(jnp.bfloat16)
-            for s in range(low, high)
-        ]
-        hot = jnp.concatenate(hot, axis=0)
-        for c in range(width // (2 * LANES)):
-            part = jnp.dot(
-                hot,
-                emb[:, c * 2 * LANES : (c + 1) * 2 * LANES],
-                preferred_element_type=jnp.float32,
-            )
-            for s in range(low, high):
-                for r in range(props // SUBLANES):
-                    for h in range(2):
-                        top = (s - low) * props + r * SUBLANES
-                        picked[s, r * across + 2 * c + h] = part[
-                            top : top + SUBLANES, h * LANES : (h + 1) * LANES
-                        ].astype(jnp.bfloat16)
+
+    def pick(low, high, loads=()):
+        wide = 2 * LANES
+        stop = (high - low) * props
+        cuts = len(loads) or 1
+        part = rows // cuts
+        for i in range(cuts):
+            if loads:
+                loads[i].wait()
+            ids = lax.broadcasted_iota(jnp.int32, (props, part), 1) + i * part
+            hot = [
+                jnp.where(ids == chosen[s][:, :1], 1.0, 0.0).astype(jnp.bfloat16)
+                for s in range(low, high)
+            ]
+            hot = jnp.concatenate(hot, axis=0)
+            for c in range(width // wide):
+                at = slice(c * wide, (c + 1) * wide)
+                term = jnp.dot(
+                    hot, emb[i * part : (i + 1) * part, at], preferred_element_type=jnp.float32
+                )
+                found[:stop, at] = term if i == 0 else found[:stop, at] + term
+        for s in range(low, high):
+            for r in range(props // SUBLANES):
+                top = (s - low) * props + r * SUBLANES
+                for c in range(across):
+                    picked[s, r * across + c] = found[
+                        top : top + SUBLANES, c * LANES : (c + 1) * LANES
+                    ].astype(jnp.bfloat16)
 
     def scatter(s):
-        def to(block, device):
-            hop = lax.rem(device - me + n, n)
+        def to(block, peer, slot):
             pltpu.make_async_remote_copy(
                 src_ref=picked.at[s, block],
-                dst_ref=arrived.at[s, hop - 1],
+                dst_ref=arrived.at[s, slot],
                 send_sem=rs_send.at[s],
                 recv_sem=rs_recv.at[s],
-                device_id=coords(device),
+                device_id=peer,
                 device_id_type=MESH,
             ).start()
 
         if spread == 1:
-
-            @pl.loop(1, n)
-            def _(hop):
-                device = lax.rem(me + hop, n)
-                to(device, device)
+            each_peer(lambda peer, slot: to(peer[0] * grp + peer[1], peer, slot))
         else:
 
             @pl.loop(0, blocks)
             def _(block):
                 @pl.when(block * spread != me)
                 def _():
-                    to(block, block * spread)
+                    device = block * spread
+                    at, turn = coords(device)
+                    step = lax.rem(at - my_pts + pts, pts)
+                    to(block, (at, turn), step * grp + lax.rem(turn - my_grp + grp, grp) - 1)
 
     def wait_for(ref, sem):
         pltpu.make_async_copy(ref, ref, sem).wait()
@@ -133,16 +162,16 @@
             block_sum[s] = total
             fetched[s, my_block] = total
 
-            @pl.loop(1, n)
-            def _(hop):
-                pltpu.make_async_remote_copy(
+            each_peer(
+                lambda peer, _: pltpu.make_async_remote_copy(
                     src_ref=block_sum.at[s],
                     dst_ref=fetched.at[s, my_block],
                     send_sem=ag_send.at[s],
                     recv_sem=ag_recv.at[s],
-                    device_id=coords(lax.rem(me + hop, n)),
+                    device_id=peer,
                     device_id_type=MESH,
                 ).start()
+            )
 
     def similarity(s):
         if spread == 1:
@@ -179,16 +208,16 @@
         gain_src[s] = row
         gain_buf[s, me] = row
 
-        @pl.loop(1, n)
-        def _(hop):
-            pltpu.make_async_remote_copy(
+        each_peer(
+            lambda peer, _: pltpu.make_async_remote_copy(
                 src_ref=gain_src.at[s],
                 dst_ref=gain_buf.at[s, me],
                 send_sem=gain_send.at[s],
                 recv_sem=gain_recv.at[s],
-                device_id=coords(lax.rem(me + hop, n)),
+                device_id=peer,
                 device_id_type=MESH,
             ).start()
+        )
 
     def take_sums(s):
         wait_for(gain_buf.at[s, pl.ds(0, n - 1)], gain_recv.at[s])
@@ -209,68 +238,72 @@
 
     cover_out[...] = jnp.zeros_like(cover_out)
     early = min(2, steps)
-    for load in loads:
-        load.wait()
-    pick(0, early)
+    pick(0, early, loads)
     pl.semaphore_wait(barrier, n - 1)
     for s in range(early):
         scatter(s)
-    pick(early, steps)
+    if early < steps:
+        pick(early, steps)
     for s in range(early):
         gather(s)
-    scatter(early)
+    if early < steps:
+        scatter(early)
     similarity(0)
+
+    def as_row(clipped):
+        column = jnp.sum(clipped, axis=1, keepdims=True)
+        return jnp.sum(jnp.where(eye, column, 0.0), axis=0, keepdims=True)
+
+    lane_blocks = [slice(i * LANES, (i + 1) * LANES) for i in range(rows // LANES)]
+    clipped = jnp.zeros((props, LANES), jnp.float32)
+    for at in lane_blocks:
+        clipped += jnp.maximum(sims[0, :, at] - best_out[:, at], 0.0)
+    send_sums(0, as_row(clipped))
+    for s in range(2, min(3, steps)):
+        gather(s)
+    for s in range(3, min(4, steps)):
+        scatter(s)
+    for s in range(1, min(2, steps)):
+        similarity(s)
 
     @pl.loop(0, steps)
     def _(s):
         slot = lax.rem(s, 2)
-        clipped = jnp.zeros((props, LANES), jnp.float32)
-        for i in range(rows // LANES):
-            at = slice(i * LANES, (i + 1) * LANES)
-            clipped += jnp.maximum(sims[slot, :, at] - best_out[:, at], 0.0)
-        column = jnp.sum(clipped, axis=1, keepdims=True)
-        row = jnp.sum(jnp.where(eye, column, 0.0), axis=0, keepdims=True)
-        cover = jnp.sum(cover_part[...], axis=1, keepdims=True)
-        send_sums(s, jnp.where(lane == props, cover, row))
-
-        @pl.when(s + 2 < steps)
-        def _():
-            gather(s + 2)
-
-        @pl.when(s + 3 < steps)
-        def _():
-            scatter(s + 3)
-
-        @pl.when(s > 0)
-        def _():
-            refresh(s - 1)
-
-        @pl.when(s + 1 < steps)
-        def _():
-            similarity(s + 1)
-
         means = take_sums(s)
         gains = jnp.sum(jnp.where(eye, means, 0.0), axis=1, keepdims=True)
         weights = (gains + 0.01) / (jnp.sum(gains, axis=0, keepdims=True) + 0.01 * props)
         weights = jnp.broadcast_to(weights, (props, LANES))
         covered = jnp.zeros((1, LANES), jnp.float32)
-        for i in range(rows // LANES):
-            at = slice(i * LANES, (i + 1) * LANES)
+        clipped = jnp.zeros((props, LANES), jnp.float32)
+        for at in lane_blocks:
             mixed = jnp.sum(sims[slot, :, at] * weights, axis=0, keepdims=True)
             best = jnp.maximum(best_out[:, at], mixed)
             best_out[:, at] = best
             covered += best
-        cover_part[...] = covered
+            clipped += jnp.maximum(sims[1 - slot, :, at] - best, 0.0)
+        cover = jnp.sum(covered, axis=1, keepdims=True)
+        send_sums(s + 1, jnp.where(lane == props, cover, as_row(clipped)))
+
+        @pl.when(s + 3 < steps)
+        def _():
+            gather(s + 3)
+
+        @pl.when(s + 4 < steps)
+        def _():
+            scatter(s + 4)
+
         gain_col[...] = jnp.broadcast_to(gains, (props, LANES))
         gain_out[pl.ds(s, 1), :] = means[:, :props]
+        refresh(s)
 
         @pl.when(s > 0)
         def _():
             keep_cover(s - 1, means)
 
-    cover = jnp.sum(cover_part[...], axis=1, keepdims=True)
-    send_sums(steps, jnp.where(lane == props, cover, 0.0))
-    refresh(steps - 1)
+        @pl.when(s + 2 < steps)
+        def _():
+            similarity(s + 2)
+
     keep_cover(steps - 1, take_sums(steps))
 
     @pl.loop(0, steps)
@@ -292,6 +325,11 @@
     @pl.loop(0, steps + 1)
     def _(s):
         wait_for(gain_buf.at[s, pl.ds(0, n - 1)], gain_send.at[s])
+
+
+def hand_over(*refs):
+    for source, target in zip(refs[:4], refs[4:]):
+        target[...] = source[...]
 
 
 def on_device(pts, grp, embeddings, best_start, bounds_start, proposals):
@@ -323,8 +361,8 @@
             pltpu.VMEM((2, props, rows), f32),
             pltpu.VMEM((steps + 1, 1, LANES), f32),
             pltpu.VMEM((steps + 1, n, 1, LANES), f32),
-            pltpu.VMEM((1, LANES), f32),
             pltpu.VMEM((props, LANES), f32),
+            pltpu.VMEM((steps * props, width), f32),
             dma((steps,)),
             dma((steps,)),
             dma((steps,)),
@@ -336,6 +374,13 @@
             collective_id=0, has_side_effects=True, vmem_limit_bytes=56 * 1024 * 1024
         ),
     )(embeddings, best_start.reshape(1, rows), bounds_start.reshape(1, rows), proposals)
+    results = (gains, cover, best, bounds)
+    gains, cover, best, bounds = pl.pallas_call(
+        hand_over,
+        out_shape=tuple(jax.ShapeDtypeStruct(x.shape, x.dtype) for x in results),
+        in_specs=[vmem] * 4,
+        out_specs=(vmem,) * 4,
+    )(*results)
     return gains, cover.reshape(steps), best.reshape(rows), bounds.reshape(rows)
 
 

time: 77.9 us -> 68.6 us (0.88)
  local copies, waits for them, and re-layouts: 5.06 us -> 0 us
  Pallas kernels: 71.7 us -> 67.6 us
    pallas_call x1, Pallas kernels: 71.7 us -> 66.3 us  [on_device(): pl.pallas_call(functools.partial(greedy_kernel, pts, grp, steps, props, r...]
    unnamed x4 -> x0, local copies, waits for them, and re-layouts: 5.06 us -> none
    pallas_call x0 -> x1, Pallas kernels: none -> 1.37 us  [on_device(): pl.pallas_call(hand_over, out_shape=tuple((jax.ShapeDtypeStruct(x.shape,...]
where the time goes in v2:
time: 68.6 us; the launch traced here: 68.3 us
  Pallas kernels  67.6 us (99%)
    pallas_call x1, Pallas kernels, on_device(): pl.pallas_call(functools.partial(greedy_kernel, pts, grp, steps, props, r...  66.3 us

profile of v2, /device:TPU:0, one launch (start us, length us, event | category | flops | bytes accessed | tf_op | source)
XLA Modules:
  0.0 68.3 jit_solution(16796323169140717786)
XLA Ops:
  0.6 66.3 %shard_map.75 = (f32[8,32]{1,0:T(8,128)}, f32[1,8]{1,0:T(1,128)}, f32[1,4096]{1,0:T(1,128)}, f32[1,4096]{1,0:T(1,128)}) custom-call(bf16[4096,1024]{1,0:T(8,128)(2,1)} %emb_hbm.1, f32[1,4096]{1,0:T(1,128)} %bitcast.5, f32[1,4096]{1,0:T(1,128)} %bitcast.6, s32[8,32]{1,0:T(8,128)} %props_in.1), custom_call_target="tpu_custom_call" | custom-call | tf_op jit(solution)/shard_map/pallas_call | solution.py:343
  66.9 1.4 %shard_map.76 = (f32[8,32]{1,0:T(8,128)}, f32[1,8]{1,0:T(1,128)}, f32[1,4096]{1,0:T(1,128)}, f32[1,4096]{1,0:T(1,128)}) custom-call(f32[8,32]{1,0:T(8,128)} %get-tuple-element.12.refs_0_, f32[1,8]{1,0:T(1,128)} %get-tuple-element.13.refs_1_, f32[1,4096]{1,0:T(1,128)} %get-tuple-element.14.refs_2_, f32[1,4096]{1,0:T(1,128)} %get-tuple-element.15.refs_3_), custom_call_target="tpu_custom_call" | custom-call | tf_op jit(solution)/shard_map/pallas_call | solution.py:378

commit v3 on v2

--- a/solution.py
+++ b/solution.py
@@ -246,8 +246,8 @@
         pick(early, steps)
     for s in range(early):
         gather(s)
-    if early < steps:
-        scatter(early)
+    for s in range(early, min(early + 2, steps)):
+        scatter(s)
     similarity(0)
 
     def as_row(clipped):
@@ -261,7 +261,7 @@
     send_sums(0, as_row(clipped))
     for s in range(2, min(3, steps)):
         gather(s)
-    for s in range(3, min(4, steps)):
+    for s in range(4, min(5, steps)):
         scatter(s)
     for s in range(1, min(2, steps)):
         similarity(s)
@@ -288,9 +288,9 @@
         def _():
             gather(s + 3)
 
-        @pl.when(s + 4 < steps)
-        def _():
-            scatter(s + 4)
+        @pl.when(s + 5 < steps)
+        def _():
+            scatter(s + 5)
 
         gain_col[...] = jnp.broadcast_to(gains, (props, LANES))
         gain_out[pl.ds(s, 1), :] = means[:, :props]

time: 68.6 us -> 66.7 us (0.972)
  Pallas kernels: 67.6 us -> 65.8 us
    pallas_call x1, Pallas kernels: 66.3 us -> 64.4 us  [on_device(): pl.pallas_call(functools.partial(greedy_kernel, pts, grp, steps, props, r...]
where the time goes in v3:
time: 66.7 us; the launch traced here: 66.4 us
  Pallas kernels  65.8 us (99%)
    pallas_call x1, Pallas kernels, on_device(): pl.pallas_call(functools.partial(greedy_kernel, pts, grp, steps, props, r...  64.4 us
    pallas_call x1, Pallas kernels, on_device(): pl.pallas_call(hand_over, out_shape=tuple((jax.ShapeDtypeStruct(x.shape,...  1.37 us

profile of v3, /device:TPU:0, one launch (start us, length us, event | category | flops | bytes accessed | tf_op | source)
XLA Modules:
  0.0 66.4 jit_solution(7469496597804714458)
XLA Ops:
  0.6 64.4 %shard_map.75 = (f32[8,32]{1,0:T(8,128)}, f32[1,8]{1,0:T(1,128)}, f32[1,4096]{1,0:T(1,128)}, f32[1,4096]{1,0:T(1,128)}) custom-call(bf16[4096,1024]{1,0:T(8,128)(2,1)} %emb_hbm.1, f32[1,4096]{1,0:T(1,128)} %bitcast.5, f32[1,4096]{1,0:T(1,128)} %bitcast.6, s32[8,32]{1,0:T(8,128)} %props_in.1), custom_call_target="tpu_custom_call" | custom-call | tf_op jit(solution)/shard_map/pallas_call | solution.py:343
  65.0 1.4 %shard_map.76 = (f32[8,32]{1,0:T(8,128)}, f32[1,8]{1,0:T(1,128)}, f32[1,4096]{1,0:T(1,128)}, f32[1,4096]{1,0:T(1,128)}) custom-call(f32[8,32]{1,0:T(8,128)} %get-tuple-element.12.refs_0_, f32[1,8]{1,0:T(1,128)} %get-tuple-element.13.refs_1_, f32[1,4096]{1,0:T(1,128)} %get-tuple-element.14.refs_2_, f32[1,4096]{1,0:T(1,128)} %get-tuple-element.15.refs_3_), custom_call_target="tpu_custom_call" | custom-call | tf_op jit(solution)/shard_map/pallas_call | solution.py:378
